TPU v7x, 128 devices: a whole 4x4x4 slice. The times are simulated.
128 devices in a mesh: dp: 8 (over z, y_hi), expert: 4 (over y_lo, core), sample: 4 (over x).
Axes of the slice: x: 4, y: 4 (y_hi: 2, y_lo: 2; y = y_hi * 2 + y_lo), z: 4, core: 2. Of those that a mesh axis runs over, the one named last changes fastest.
Arguments:
- tokens: bfloat16 [2560, 4096], P(('dp', 'expert', 'sample')), may hold values from -6 to 6
- cotangent: bfloat16 [2560, 4096], P(('dp', 'expert', 'sample')), may hold values from -6 to 6
- routes: int32 [2560, 2], P(('dp', 'expert', 'sample')), may hold values from 0 to 7, all different within a row; in each aligned block of 20 rows (0 to 19, 20 to 39, ...) at most 6 rows name the same one
- gate_weights: float32 [2560, 2], P(('dp', 'expert', 'sample')), may hold values from 0.1 to 1
- lengths: int32 [32, 4], P(('dp', 'expert'), 'sample'), may hold values from 1 to 20
- rewards: int32 [32, 4], P(('dp', 'expert'), 'sample'), may hold values from -48 to 48
- w_gate: bfloat16 [8, 8192, 4096], P('expert', ('dp', 'sample')), may hold values from -0.09375 to 0.09375
- w_up: bfloat16 [8, 8192, 4096], P('expert', ('dp', 'sample')), may hold values from -0.09375 to 0.09375
- w_down: bfloat16 [8, 8192, 4096], P('expert', ('dp', 'sample')), may hold values from -0.0625 to 0.0625
Outputs:
- grad_tokens: bfloat16 [2560, 4096], P(('dp', 'expert', 'sample'))
- grad_w_gate: bfloat16 [8, 8192, 4096], P('expert', ('dp', 'sample'))
- grad_w_up: bfloat16 [8, 8192, 4096], P('expert', ('dp', 'sample'))
- grad_w_down: bfloat16 [8, 8192, 4096], P('expert', ('dp', 'sample'))
Inputs may be any that keep to these rules, and one draw needn't show every extreme that they name: `routes`: each row names 2 different experts; among the rows of one device no expert is named by more than 6 rows, and in every draw some device's rows name some expert exactly 6 times.
All inputs are finite; a program needn't handle non-finite values.
Results may differ from a plain program's by a relative error of at most 0.025.
Values may be sent and summed in bfloat16 or wider, within the bound.
A program may use at most 192 MiB of HBM per device.

v0:
```python
import jax
import jax.numpy as jnp
from jax import lax
from jax.sharding import PartitionSpec as P

CAP = 6


def silu_parts(pre_gate):
    gate_prob = jax.nn.sigmoid(pre_gate)
    return (pre_gate * gate_prob, gate_prob * (1.0 + pre_gate * (1.0 - gate_prob)))


def expert_rows(inputs, grads_out, w_gate, w_up, w_down):
    pre_gate = jnp.einsum("rjcd,jfd->rjcf", inputs, w_gate, preferred_element_type=jnp.float32)
    pre_up = jnp.einsum("rjcd,jfd->rjcf", inputs, w_up, preferred_element_type=jnp.float32)
    active, derivative = silu_parts(pre_gate)
    hidden = (active * pre_up).astype(jnp.bfloat16)
    grad_hidden = jnp.einsum(
        "rjcd,jfd->rjcf", grads_out, w_down, preferred_element_type=jnp.float32
    )
    grad_gate = (grad_hidden * pre_up * derivative).astype(jnp.bfloat16)
    grad_up = (grad_hidden * active).astype(jnp.bfloat16)
    return (hidden, grad_gate, grad_up)


def weight_terms(inputs, grads_out, hidden, grad_gate, grad_up):
    term_gate = jnp.einsum("rjcf,rjcd->jfd", grad_gate, inputs, preferred_element_type=jnp.float32)
    term_up = jnp.einsum("rjcf,rjcd->jfd", grad_up, inputs, preferred_element_type=jnp.float32)
    term_down = jnp.einsum("rjcf,rjcd->jfd", hidden, grads_out, preferred_element_type=jnp.float32)
    return (term_gate, term_up, term_down)


def input_terms(grad_gate, grad_up, w_gate, w_up):
    from_gate = jnp.einsum("rjcf,jfd->rjcd", grad_gate, w_gate, preferred_element_type=jnp.float32)
    from_up = jnp.einsum("rjcf,jfd->rjcd", grad_up, w_up, preferred_element_type=jnp.float32)
    return from_gate + from_up


def local(tokens, cotangent, routes, gate_weights, lengths, rewards, w_gate, w_up, w_down):
    samples = lax.axis_size("sample")
    own_reward = rewards.astype(jnp.float32) * 0.0625
    reward_total = lax.psum(own_reward, "sample")
    advantage = own_reward - (reward_total - own_reward) / (samples - 1)
    token_count = tokens.shape[0]
    model_width = tokens.shape[1]
    choices_per = routes.shape[1]
    local_experts = w_gate.shape[0]
    expert_groups = lax.axis_size("expert")
    all_experts = local_experts * expert_groups
    positions = jnp.arange(token_count, dtype=jnp.int32)
    weight_row = jnp.where(positions < lengths[0, 0], -advantage[0, 0], jnp.zeros((), jnp.float32))
    pair_scale = (gate_weights * weight_row[:, None]).reshape(-1)
    pair_expert = routes.reshape(-1)
    member = (pair_expert[:, None] == jnp.arange(all_experts, dtype=jnp.int32)[None, :]).astype(
        jnp.int32
    )
    earlier = jnp.sum((jnp.cumsum(member, axis=0) - member) * member, axis=1)
    target = pair_expert * CAP + earlier
    slot_ids = jnp.arange(all_experts * CAP, dtype=jnp.int32)
    placed = target[:, None] == slot_ids[None, :]
    chosen = jnp.sum(
        placed.reshape(token_count, choices_per, -1).astype(jnp.float32), axis=1
    ).astype(jnp.bfloat16)
    slot_scale = jnp.sum(jnp.where(placed, pair_scale[:, None], jnp.zeros((), jnp.float32)), axis=0)
    sent_inputs = jnp.dot(chosen.T, tokens, preferred_element_type=jnp.float32).astype(jnp.bfloat16)
    sent_cotangent = jnp.dot(chosen.T, cotangent, preferred_element_type=jnp.float32)
    sent_grads = (sent_cotangent * slot_scale[:, None]).astype(jnp.bfloat16)
    layout = (expert_groups, local_experts, CAP, model_width)
    arrived_inputs, arrived_grads = (
        lax.all_to_all(
            sent_inputs.reshape(layout), "expert", split_axis=0, concat_axis=0, tiled=True
        ),
        lax.all_to_all(
            sent_grads.reshape(layout), "expert", split_axis=0, concat_axis=0, tiled=True
        ),
    )
    piece_inputs = lax.all_gather(arrived_inputs, ("dp", "sample"), axis=0, tiled=True)
    piece_grads = lax.all_gather(arrived_grads, ("dp", "sample"), axis=0, tiled=True)
    hidden, grad_gate, grad_up = expert_rows(piece_inputs, piece_grads, w_gate, w_up, w_down)
    add_gate, add_up, add_down = weight_terms(piece_inputs, piece_grads, hidden, grad_gate, grad_up)
    rows_part = input_terms(grad_gate, grad_up, w_gate, w_up)
    partial_value = rows_part
    term_gate, term_up, term_down, partial_value = (add_gate, add_up, add_down, partial_value)
    row_sums = lax.psum_scatter(
        partial_value.astype(jnp.bfloat16), ("dp", "sample"), scatter_dimension=0, tiled=True
    )
    returned = lax.all_to_all(row_sums, "expert", split_axis=0, concat_axis=0, tiled=True)
    flat_back = returned.reshape(all_experts * CAP, model_width)
    grad_tokens = jnp.dot(chosen, flat_back, preferred_element_type=jnp.float32).astype(
        jnp.bfloat16
    )
    return (
        grad_tokens,
        term_gate.astype(jnp.bfloat16),
        term_up.astype(jnp.bfloat16),
        term_down.astype(jnp.bfloat16),
    )


def solution(mesh):
    in_specs = (
        P(("dp", "expert", "sample"), None),
        P(("dp", "expert", "sample"), None),
        P(("dp", "expert", "sample"), None),
        P(("dp", "expert", "sample"), None),
        P(("dp", "expert"), "sample"),
        P(("dp", "expert"), "sample"),
        P("expert", ("dp", "sample"), None),
        P("expert", ("dp", "sample"), None),
        P("expert", ("dp", "sample"), None),
    )
    out_specs = (
        P(("dp", "expert", "sample"), None),
        P("expert", ("dp", "sample"), None),
        P("expert", ("dp", "sample"), None),
        P("expert", ("dp", "sample"), None),
    )
    return jax.shard_map(local, mesh=mesh, in_specs=in_specs, out_specs=out_specs, check_vma=False)
```

profile of v0, /device:TPU:1, one launch (start us, length us, event | category | flops | bytes accessed | tf_op | source)
XLA Modules:
  0.0 765.0 jit_solution(14036604109499341105)
XLA Ops:
  7.2 0.8 copy.82
  8.6 0.7 multiply_add_fusion
  10.4 10.8 %all_to_all.15 = bf16[4,2,6,4096]{3,1,2,0:T(2,128)(2,1)} all-to-all(bf16[4,2,6,4096]{3,1,2,0:T(2,128)(2,1)S(1)} %copy.88), channel_id=1, replica_groups=mesh['dp'=8,'expert'=4,'sample'=4] {'expert'}, dimensions={0} | all-to-all | bytes 786432 | tf_op jit(solution)/shard_map/all_to_all | solution.py:71
  22.0 9.1 %psum.7 = f32[1,1]{1,0:T(1,128)} all-reduce(f32[1,1]{1,0:T(1,128)S(6)} %mul.63), channel_id=1, replica_groups=mesh['dp'=8,'expert'=4,'sample'=4] {'sample'}, use_global_device_ids=true, to_apply=%region_3.4 | all-reduce | flops 1 | bytes 8 | tf_op jit(solution)/shard_map/psum | solution.py:43
  32.4 0.7 broadcast_multiply_fusion
  33.3 1.2 fusion.19
  35.1 12.8 %all_to_all.16 = bf16[4,2,6,4096]{3,1,2,0:T(2,128)(2,1)} all-to-all(bf16[4,2,6,4096]{3,1,2,0:T(2,128)(2,1)S(1)} %copy.86), channel_id=1, replica_groups=mesh['dp'=8,'expert'=4,'sample'=4] {'expert'}, dimensions={0} | all-to-all | bytes 786432 | tf_op jit(solution)/shard_map/all_to_all | solution.py:74
  48.5 103.7 %all-gather.5.cloned.1.call-done = bf16[128,2,6,4096]{3,1,2,0:T(2,128)(2,1)} async-done(((bf16[4,2,6,4096]{3,1,2,0:T(2,128)(2,1)}), bf16[128,2,6,4096]{3,1,2,0:T(2,128)(2,1)}) %all-gather.5.cloned.1.call-update) | async-done | bytes 12582928 | tf_op jit(solution)/shard_map/all_gather | solution.py:78
  152.2 14.3 %fusion.9 = f32[2,128,6,256]{3,1,2,0:T(8,128)} fusion(bf16[128,2,6,4096]{3,1,2,0:T(2,128)(2,1)} %all-gather.5.cloned.1.call-done, bf16[2,256,4096]{2,1,0:T(8,128)(2,1)} %param.15), kind=kOutput, calls=%fused_computation.13 | convolution fusion | flops 3221225472 | bytes 18350080 | tf_op jit(solution)/shard_map/rjcd,jfd->rjcf/dot_general | solution.py:15
  166.5 13.2 %fusion.11 = f32[2,128,6,256]{3,1,2,0:T(8,128)} fusion(bf16[128,2,6,4096]{3,1,2,0:T(2,128)(2,1)} %all-gather.5.cloned.1.call-done, bf16[2,256,4096]{2,1,0:T(8,128)(2,1)S(1)} %copy-done.2), kind=kOutput, calls=%fused_computation.15 | convolution fusion | flops 3221225472 | bytes 18350080 | tf_op jit(solution)/shard_map/rjcd,jfd->rjcf/dot_general | solution.py:16
  179.7 101.9 %all-gather.3.cloned.1.call-done = bf16[128,2,6,4096]{3,1,2,0:T(2,128)(2,1)} async-done(((bf16[4,2,6,4096]{3,1,2,0:T(2,128)(2,1)}), bf16[128,2,6,4096]{3,1,2,0:T(2,128)(2,1)}) %all-gather.3.cloned.1.call-update) | async-done | bytes 12582928 | tf_op jit(solution)/shard_map/all_gather | solution.py:79
  281.6 14.4 %fusion.34 = (bf16[128,2,6,256]{3,0,2,1:T(8,128)(2,1)S(1)}, bf16[128,2,6,256]{3,0,2,1:T(8,128)(2,1)S(1)}) fusion(f32[2,128,6,256]{3,1,2,0:T(8,128)} %fusion.9, f32[2,128,6,256]{3,1,2,0:T(8,128)} %fusion.11, bf16[2,256,4096]{2,1,0:T(8,128)(2,1)} %param.17, bf16[128,2,6,4096]{3,1,2,0:T(2,128)(2,1)} %all-gather.3.cloned.1.call-done), kind=kOutput, calls=%fused_computation.41 | convolution fusion | flops 3226337280 | bytes 21495808 | tf_op jit(solution)/shard_map/rjcd,jfd->rjcf/dot_general | solution.py:19
  296.0 12.3 %fusion.20 = f32[2,128,6,4096]{3,1,2,0:T(8,128)} fusion(bf16[128,2,6,256]{3,0,2,1:T(8,128)(2,1)S(1)} %get-tuple-element.5, bf16[2,256,4096]{2,1,0:T(8,128)(2,1)} %param.15), kind=kOutput, calls=%fused_computation.21 | convolution fusion | flops 3221225472 | bytes 30146560 | tf_op jit(solution)/shard_map/rjcf,jfd->rjcd/dot_general | solution.py:35
  308.3 15.7 %fusion = bf16[128,2,6,4096]{3,0,2,1:T(8,128)(2,1)} fusion(f32[2,128,6,4096]{3,1,2,0:T(8,128)} %fusion.20, bf16[128,2,6,256]{3,0,2,1:T(8,128)(2,1)S(1)} %get-tuple-element.4, bf16[2,256,4096]{2,1,0:T(8,128)(2,1)} %param.16), kind=kOutput, calls=%fused_computation.1 | convolution fusion | flops 3233808384 | bytes 42729472 | tf_op jit(solution)/shard_map/rjcf,jfd->rjcd/dot_general | solution.py:36
  324.1 0.6 copy-done.3
  324.7 0.6 dynamic-slice
  326.0 21.9 %bitcast_convert_fusion.1 = bf16[2,256,4096]{2,1,0:T(8,128)(2,1)} fusion(bf16[128,2,6,256]{3,0,2,1:T(8,128)(2,1)S(1)} %get-tuple-element.4, bf16[128,2,6,4096]{3,1,2,0:T(2,128)(2,1)} %all-gather.5.cloned.1.call-done), kind=kOutput, calls=%fused_computation.7 | convolution fusion | flops 3223322624 | bytes 17563648 | tf_op jit(solution)/shard_map/rjcf,rjcd->jfd/dot_general | solution.py:29
  347.9 22.2 %bitcast_convert_fusion = bf16[2,256,4096]{2,1,0:T(8,128)(2,1)} fusion(bf16[128,2,6,4096]{3,1,2,0:T(2,128)(2,1)} %all-gather.3.cloned.1.call-done, f32[2,128,6,256]{3,1,2,0:T(8,128)S(1)} %copy-done.5, f32[2,128,6,256]{3,1,2,0:T(8,128)S(1)} %copy-done.4), kind=kOutput, calls=%fused_computation.6 | convolution fusion | flops 3225681920 | bytes 19922944 | tf_op jit(solution)/shard_map/rjcf,rjcd->jfd/dot_general | solution.py:30
  370.1 339.9 %all-reduce.3.cloned.1.call-done = bf16[128,2,6,4096]{3,0,2,1:T(8,128)(2,1)} async-done(((bf16[128,2,6,4096]{3,0,2,1:T(8,128)(2,1)}), bf16[128,2,6,4096]{3,0,2,1:T(8,128)(2,1)}) %all-reduce.3.cloned.1.call-update) | async-done | bytes 12582928
  710.0 1.4 constant_dynamic-slice_fusion
  711.4 1.1 copy.91
  712.5 22.2 %all-to-all-start.2 = ((bf16[4,2,6,4096]{3,1,2,0:T(2,128)(2,1)}), bf16[4,2,6,4096]{3,1,2,0:T(2,128)(2,1)S(1)}, u32[]{:S(2)}, u32[]{:S(2)}) async-start(bf16[4,2,6,4096]{3,1,2,0:T(2,128)(2,1)} %copy.91), calls=%async_computation.2 | async-start | bytes 786432 | tf_op jit(solution)/shard_map/all_to_all | solution.py:88
  734.7 22.0 %bitcast_convert_fusion.2 = bf16[2,256,4096]{2,1,0:T(8,128)(2,1)} fusion(bf16[128,2,6,256]{3,0,2,1:T(8,128)(2,1)S(1)} %get-tuple-element.5, bf16[128,2,6,4096]{3,1,2,0:T(2,128)(2,1)} %all-gather.5.cloned.1.call-done), kind=kOutput, calls=%fused_computation.8 | convolution fusion | flops 3223322624 | bytes 17563648 | tf_op jit(solution)/shard_map/rjcf,rjcd->jfd/dot_general | solution.py:28
  757.1 0.9 convolution_convert_fusion.1
  (38 shorter events, 3.6 us)
Async XLA Ops:
  7.2 2.4 copy-start
  7.2 145.0 %all-gather.5.cloned.1.call-start = ((), (), s32[]{:S(2)}) async-start(), calls=%async_computation.4 | async-start | bytes 12976128 | tf_op jit(solution)/shard_map/all_gather | solution.py:78
  21.3 260.3 %all-gather.3.cloned.1.call-start = ((), (), s32[]{:S(2)}) async-start(), calls=%async_computation.3 | async-start | bytes 12976128 | tf_op jit(solution)/shard_map/all_gather | solution.py:79
  48.0 662.1 %all-reduce.3.cloned.1.call-start = ((), (), s32[]{:S(2)}) async-start(), calls=%async_computation.5 | async-start | bytes 25165824
  152.2 14.3 %copy-start.2 = (bf16[2,256,4096]{2,1,0:T(8,128)(2,1)S(1)}, bf16[2,256,4096]{2,1,0:T(8,128)(2,1)}, u32[]{:S(2)}) copy-start(bf16[2,256,4096]{2,1,0:T(8,128)(2,1)} %param.16) | copy-start | bytes 12582916
  324.0 0.7 copy-start.3
  325.9 22.0 %copy-start.4 = (f32[2,128,6,256]{3,1,2,0:T(8,128)S(1)}, f32[2,128,6,256]{3,1,2,0:T(8,128)}, u32[]{:S(2)}) copy-start(f32[2,128,6,256]{3,1,2,0:T(8,128)} %fusion.9) | copy-start | bytes 4718596
  325.9 22.0 %copy-start.5 = (f32[2,128,6,256]{3,1,2,0:T(8,128)S(1)}, f32[2,128,6,256]{3,1,2,0:T(8,128)}, u32[]{:S(2)}) copy-start(f32[2,128,6,256]{3,1,2,0:T(8,128)} %fusion.11) | copy-start | bytes 4718596
  712.5 44.2 %all-to-all-start.2 = ((bf16[4,2,6,4096]{3,1,2,0:T(2,128)(2,1)}), bf16[4,2,6,4096]{3,1,2,0:T(2,128)(2,1)S(1)}, u32[]{:S(2)}, u32[]{:S(2)}) async-start(bf16[4,2,6,4096]{3,1,2,0:T(2,128)(2,1)} %copy.91), calls=%async_computation.2 | async-start | bytes 786432 | tf_op jit(solution)/shard_map/all_to_all | solution.py:88
  734.7 23.2 %copy-start.1 = (bf16[20,4096]{1,0:T(8,128)(2,1)S(1)}, bf16[20,4096]{1,0:T(8,128)(2,1)}, u32[]{:S(2)}) copy-start(bf16[20,4096]{1,0:T(8,128)(2,1)} %param.9) | copy-start | bytes 491524
Sparse Core Ops, SparseCore 0:
  21.4 130.7 all-gather.4
  155.2 126.3 all-gather.2
  324.2 385.8 all-reduce.2
where the time goes:
time: 768 us; the launch traced here: 765 us
  waiting for transfers between devices  546 us (71%)
  matrix products  138 us (18%)
  blocking collectives  32.7 us (4%)
  starting transfers between devices  22.8 us (3%)
  between operations  17 us (2%)
    unnamed x4, waiting for transfers between devices  340 us
    all_gather x1, waiting for transfers between devices, local(): lax.all_gather(arrived_inputs, ('dp', 'sample'), axis=0, tiled=True)  104 us
    all_gather x1, waiting for transfers between devices, local(): lax.all_gather(arrived_grads, ('dp', 'sample'), axis=0, tiled=True)  102 us
    dot_general x1, matrix products, weight_terms(): jnp.einsum('rjcf,rjcd->jfd', hidden, grads_out, preferred_element_type=jn...  22.2 us
    all_to_all x1, starting transfers between devices, local(): lax.all_to_all(row_sums, 'expert', split_axis=0, concat_axis=0, tiled=True)  22.2 us
    dot_general x1, matrix products, weight_terms(): jnp.einsum('rjcf,rjcd->jfd', grad_gate, inputs, preferred_element_type=jn...  22 us
    dot_general x1, matrix products, weight_terms(): jnp.einsum('rjcf,rjcd->jfd', grad_up, inputs, preferred_element_type=jnp....  21.9 us
    dot_general x1, matrix products, input_terms(): jnp.einsum('rjcf,jfd->rjcd', grad_up, w_up, preferred_element_type=jnp.fl...  15.7 us
  transfers between devices with their start and end apart: 4, of which 3 were waited for; matrix products, arithmetic and copies ran while one was open for 13% of the time, Pallas kernels for 0%

commit v1 on v0

--- a/solution.py
+++ b/solution.py
@@ -75,8 +75,16 @@
             sent_grads.reshape(layout), "expert", split_axis=0, concat_axis=0, tiled=True
         ),
     )
-    piece_inputs = lax.all_gather(arrived_inputs, ("dp", "sample"), axis=0, tiled=True)
-    piece_grads = lax.all_gather(arrived_grads, ("dp", "sample"), axis=0, tiled=True)
+    piece_inputs, piece_grads = jnp.split(
+        lax.all_gather(
+            jnp.concatenate([arrived_inputs, arrived_grads], axis=1),
+            ("dp", "sample"),
+            axis=0,
+            tiled=True,
+        ),
+        [arrived_inputs.shape[1]],
+        axis=1,
+    )
     hidden, grad_gate, grad_up = expert_rows(piece_inputs, piece_grads, w_gate, w_up, w_down)
     add_gate, add_up, add_down = weight_terms(piece_inputs, piece_grads, hidden, grad_gate, grad_up)
     rows_part = input_terms(grad_gate, grad_up, w_gate, w_up)

time: 768 us -> 803 us (1.046)
  local copies, waits for them, and re-layouts: 6.55 us -> 40 us
  blocking collectives: 32.7 us -> 19.5 us
    split x0 -> x1, local copies, waits for them, and re-layouts: none -> 32.7 us  [local(): jnp.split(lax.all_gather(jnp.concatenate([arrived_inputs, arrived_grads],...]
    all_to_all x1 -> x0, blocking collectives: 12.8 us -> none  [local(): lax.all_to_all(sent_grads.reshape(layout), 'expert', split_axis=0, concat...]
    all_gather x2 -> x1, waiting for transfers between devices: 206 us -> 207 us  [local(): lax.all_gather(jnp.concatenate([arrived_inputs, arrived_grads], axis=1),...]
    unnamed x4 -> x3, waiting for transfers between devices: 340 us -> 340 us
  transfers between devices with their start and end apart: 4 -> 4, of which waited for: 3 -> 3; matrix products, arithmetic and copies ran while one was open for 13% -> 9% of each run, Pallas kernels for 0% -> 0%
where the time goes in v1:
time: 803 us; the launch traced here: 799 us
  waiting for transfers between devices  552 us (69%)
  matrix products  138 us (17%)
  local copies, waits for them, and re-layouts  40 us (5%)
  starting transfers between devices  28.3 us (4%)
  blocking collectives  19.5 us (2%)
  between operations  17.4 us (2%)
    unnamed x3, waiting for transfers between devices  340 us
    all_gather x1, waiting for transfers between devices, local(): lax.all_gather(jnp.concatenate([arrived_inputs, arrived_grads], axis=1),...  207 us
    split x1, local copies, waits for them, and re-layouts, local(): jnp.split(lax.all_gather(jnp.concatenate([arrived_inputs, arrived_grads],...  32.7 us
    dot_general x1, matrix products, weight_terms(): jnp.einsum('rjcf,rjcd->jfd', hidden, grads_out, preferred_element_type=jn...  22.2 us
    all_to_all x1, starting transfers between devices, local(): lax.all_to_all(row_sums, 'expert', split_axis=0, concat_axis=0, tiled=True)  22.2 us
    dot_general x1, matrix products, weight_terms(): jnp.einsum('rjcf,rjcd->jfd', grad_gate, inputs, preferred_element_type=jn...  21.9 us
    dot_general x1, matrix products, weight_terms(): jnp.einsum('rjcf,rjcd->jfd', grad_up, inputs, preferred_element_type=jnp....  21.9 us
  transfers between devices with their start and end apart: 4, of which 3 were waited for; matrix products, arithmetic and copies ran while one was open for 9% of the time, Pallas kernels for 0%

profile of v1, /device:TPU:1, one launch (start us, length us, event | category | flops | bytes accessed | tf_op | source)
XLA Modules:
  0.0 799.0 jit_solution(10697910211671928970)
XLA Ops:
  7.9 0.8 copy.69
  9.2 9.8 %psum.7 = f32[1,1]{1,0:T(1,128)} all-reduce(f32[1,1]{1,0:T(1,128)S(6)} %mul.63), channel_id=1, replica_groups=mesh['dp'=8,'expert'=4,'sample'=4] {'sample'}, use_global_device_ids=true, to_apply=%region_3.4 | all-reduce | flops 1 | bytes 8 | tf_op jit(solution)/shard_map/psum | solution.py:43
  21.2 0.7 multiply_add_fusion
  22.7 1.2 copy.74
  23.8 6.1 all-to-all-start.1
  30.0 1.2 convolution_convert_fusion
  31.7 4.7 all-to-all-done.1
  36.4 9.7 %all_to_all.15 = bf16[4,2,6,4096]{3,1,2,0:T(2,128)(2,1)S(1)} all-to-all(bf16[4,2,6,4096]{3,1,2,0:T(2,128)(2,1)S(1)} %copy.72), channel_id=1, replica_groups=mesh['dp'=8,'expert'=4,'sample'=4] {'expert'}, dimensions={0} | all-to-all | bytes 786432 | tf_op jit(solution)/shard_map/all_to_all | solution.py:71
  46.1 1.7 pad_maximum_fusion
  47.9 206.6 %all-gather.2.cloned.1.call-done = bf16[128,4,6,4096]{3,1,2,0:T(4,128)(2,1)} async-done(((bf16[4,4,6,4096]{3,1,2,0:T(4,128)(2,1)}), bf16[128,4,6,4096]{3,1,2,0:T(4,128)(2,1)}) %all-gather.2.cloned.1.call-update) | async-done | bytes 25165840 | tf_op jit(solution)/shard_map/all_gather | solution.py:79
  254.5 32.7 %fusion.42 = (bf16[128,2,6,4096]{3,1,2,0:T(2,128)(2,1)}, bf16[128,2,6,4096]{3,1,2,0:T(2,128)(2,1)}) fusion(bf16[128,4,6,4096]{3,1,2,0:T(4,128)(2,1)} %all-gather.2.cloned.1.call-done), kind=kLoop, calls=%fused_computation.59 | loop fusion | bytes 50331648 | tf_op jit(solution)/shard_map/split | solution.py:78
  287.3 13.0 %fusion.9 = f32[2,128,6,256]{3,1,2,0:T(8,128)} fusion(bf16[128,2,6,4096]{3,1,2,0:T(2,128)(2,1)} %get-tuple-element.5, bf16[2,256,4096]{2,1,0:T(8,128)(2,1)S(1)} %copy-done.2), kind=kOutput, calls=%fused_computation.13 | convolution fusion | flops 3221225472 | bytes 18350080 | tf_op jit(solution)/shard_map/rjcd,jfd->rjcf/dot_general | solution.py:15
  300.3 14.3 %fusion.11 = f32[2,128,6,256]{3,1,2,0:T(8,128)} fusion(bf16[128,2,6,4096]{3,1,2,0:T(2,128)(2,1)} %get-tuple-element.5, bf16[2,256,4096]{2,1,0:T(8,128)(2,1)} %param.16), kind=kOutput, calls=%fused_computation.15 | convolution fusion | flops 3221225472 | bytes 18350080 | tf_op jit(solution)/shard_map/rjcd,jfd->rjcf/dot_general | solution.py:16
  314.6 14.4 %fusion.34 = (bf16[128,2,6,256]{3,0,2,1:T(8,128)(2,1)S(1)}, bf16[128,2,6,256]{3,0,2,1:T(8,128)(2,1)S(1)}) fusion(f32[2,128,6,256]{3,1,2,0:T(8,128)} %fusion.9, f32[2,128,6,256]{3,1,2,0:T(8,128)} %fusion.11, bf16[2,256,4096]{2,1,0:T(8,128)(2,1)} %param.17, bf16[128,2,6,4096]{3,1,2,0:T(2,128)(2,1)} %get-tuple-element.4), kind=kOutput, calls=%fused_computation.41 | convolution fusion | flops 3226337280 | bytes 21495808 | tf_op jit(solution)/shard_map/rjcd,jfd->rjcf/dot_general | solution.py:19
  329.0 12.2 %fusion.20 = f32[2,128,6,4096]{3,1,2,0:T(8,128)} fusion(bf16[128,2,6,256]{3,0,2,1:T(8,128)(2,1)S(1)} %get-tuple-element.7, bf16[2,256,4096]{2,1,0:T(8,128)(2,1)} %param.15), kind=kOutput, calls=%fused_computation.21 | convolution fusion | flops 3221225472 | bytes 30146560 | tf_op jit(solution)/shard_map/rjcf,jfd->rjcd/dot_general | solution.py:35
  341.2 16.0 %fusion = bf16[128,2,6,4096]{3,0,2,1:T(8,128)(2,1)} fusion(f32[2,128,6,4096]{3,1,2,0:T(8,128)} %fusion.20, bf16[128,2,6,256]{3,0,2,1:T(8,128)(2,1)S(1)} %get-tuple-element.6, bf16[2,256,4096]{2,1,0:T(8,128)(2,1)} %param.16), kind=kOutput, calls=%fused_computation.1 | convolution fusion | flops 3233808384 | bytes 42729472 | tf_op jit(solution)/shard_map/rjcf,jfd->rjcd/dot_general | solution.py:36
  359.2 21.9 %bitcast_convert_fusion.1 = bf16[2,256,4096]{2,1,0:T(8,128)(2,1)} fusion(bf16[128,2,6,256]{3,0,2,1:T(8,128)(2,1)S(1)} %get-tuple-element.6, bf16[128,2,6,4096]{3,1,2,0:T(2,128)(2,1)} %get-tuple-element.5), kind=kOutput, calls=%fused_computation.7 | convolution fusion | flops 3223322624 | bytes 17563648 | tf_op jit(solution)/shard_map/rjcf,rjcd->jfd/dot_general | solution.py:29
  381.1 22.2 %bitcast_convert_fusion = bf16[2,256,4096]{2,1,0:T(8,128)(2,1)} fusion(bf16[128,2,6,4096]{3,1,2,0:T(2,128)(2,1)} %get-tuple-element.4, f32[2,128,6,256]{3,1,2,0:T(8,128)S(1)} %copy-done.5, f32[2,128,6,256]{3,1,2,0:T(8,128)S(1)} %copy-done.4), kind=kOutput, calls=%fused_computation.6 | convolution fusion | flops 3225681920 | bytes 19922944 | tf_op jit(solution)/shard_map/rjcf,rjcd->jfd/dot_general | solution.py:30
  403.3 340.4 %all-reduce.3.cloned.1.call-done = bf16[128,2,6,4096]{3,0,2,1:T(8,128)(2,1)} async-done(((bf16[128,2,6,4096]{3,0,2,1:T(8,128)(2,1)}), bf16[128,2,6,4096]{3,0,2,1:T(8,128)(2,1)}) %all-reduce.3.cloned.1.call-update) | async-done | bytes 12582928
  743.7 1.4 constant_dynamic-slice_fusion
  745.1 1.1 copy.77
  746.2 22.2 %all-to-all-start.2 = ((bf16[4,2,6,4096]{3,1,2,0:T(2,128)(2,1)}), bf16[4,2,6,4096]{3,1,2,0:T(2,128)(2,1)S(1)}, u32[]{:S(2)}, u32[]{:S(2)}) async-start(bf16[4,2,6,4096]{3,1,2,0:T(2,128)(2,1)} %copy.77), calls=%async_computation.2 | async-start | bytes 786432 | tf_op jit(solution)/shard_map/all_to_all | solution.py:96
  768.4 21.9 %bitcast_convert_fusion.2 = bf16[2,256,4096]{2,1,0:T(8,128)(2,1)} fusion(bf16[128,2,6,256]{3,0,2,1:T(8,128)(2,1)S(1)} %get-tuple-element.7, bf16[128,2,6,4096]{3,1,2,0:T(2,128)(2,1)} %get-tuple-element.5), kind=kOutput, calls=%fused_computation.8 | convolution fusion | flops 3223322624 | bytes 17563648 | tf_op jit(solution)/shard_map/rjcf,rjcd->jfd/dot_general | solution.py:28
  790.7 0.9 convolution_convert_fusion.1
  (38 shorter events, 4.4 us)
Async XLA Ops:
  7.2 15.1 %copy-start = (bf16[20,4096]{1,0:T(8,128)(2,1)S(1)}, bf16[20,4096]{1,0:T(8,128)(2,1)}, u32[]{:S(2)}) copy-start(bf16[20,4096]{1,0:T(8,128)(2,1)} %param.10) | copy-start | bytes 491524
  23.8 12.6 %all-to-all-start.1 = ((bf16[4,2,6,4096]{3,1,2,0:T(2,128)(2,1)}), bf16[4,2,6,4096]{3,1,2,0:T(2,128)(2,1)S(1)}, u32[]{:S(2)}, u32[]{:S(2)}) async-start(bf16[4,2,6,4096]{3,1,2,0:T(2,128)(2,1)} %copy.74), calls=%async_computation.1 | async-start | bytes 786432 | tf_op jit(solution)/shard_map/all_to_all | solution.py:74
  30.0 224.6 %all-gather.2.cloned.1.call-start = ((), (), s32[]{:S(2)}) async-start(), calls=%async_computation.3 | async-start | bytes 25952256 | tf_op jit(solution)/shard_map/all_gather | solution.py:79
  47.8 695.9 %all-reduce.3.cloned.1.call-start = ((), (), s32[]{:S(2)}) async-start(), calls=%async_computation.4 | async-start | bytes 25165824
  254.5 32.7 %copy-start.2 = (bf16[2,256,4096]{2,1,0:T(8,128)(2,1)S(1)}, bf16[2,256,4096]{2,1,0:T(8,128)(2,1)}, u32[]{:S(2)}) copy-start(bf16[2,256,4096]{2,1,0:T(8,128)(2,1)} %param.15) | copy-start | bytes 12582916
  357.3 0.7 copy-start.3
  359.2 22.0 %copy-start.4 = (f32[2,128,6,256]{3,1,2,0:T(8,128)S(1)}, f32[2,128,6,256]{3,1,2,0:T(8,128)}, u32[]{:S(2)}) copy-start(f32[2,128,6,256]{3,1,2,0:T(8,128)} %fusion.9) | copy-start | bytes 4718596
  359.2 22.0 %copy-start.5 = (f32[2,128,6,256]{3,1,2,0:T(8,128)S(1)}, f32[2,128,6,256]{3,1,2,0:T(8,128)}, u32[]{:S(2)}) copy-start(f32[2,128,6,256]{3,1,2,0:T(8,128)} %fusion.11) | copy-start | bytes 4718596
  746.2 44.1 %all-to-all-start.2 = ((bf16[4,2,6,4096]{3,1,2,0:T(2,128)(2,1)}), bf16[4,2,6,4096]{3,1,2,0:T(2,128)(2,1)S(1)}, u32[]{:S(2)}, u32[]{:S(2)}) async-start(bf16[4,2,6,4096]{3,1,2,0:T(2,128)(2,1)} %copy.77), calls=%async_computation.2 | async-start | bytes 786432 | tf_op jit(solution)/shard_map/all_to_all | solution.py:96
  768.4 23.2 %copy-start.1 = (bf16[20,4096]{1,0:T(8,128)(2,1)S(1)}, bf16[20,4096]{1,0:T(8,128)(2,1)}, u32[]{:S(2)}) copy-start(bf16[20,4096]{1,0:T(8,128)(2,1)} %param.10) | copy-start | bytes 491524
Sparse Core Ops, SparseCore 0:
  48.0 206.5 all-gather.1
  357.4 386.2 all-reduce.2
